TPU v7x, 32 devices: a whole 2x2x4 slice. The times are simulated.
32 devices in a mesh: parts: 2 (over y), samp: 16 (over z, x, core).
Axes of the slice: x: 2, y: 2, z: 4, core: 2. Of those that a mesh axis runs over, the one named last changes fastest.
Arguments:
- expression: bfloat16 [1024, 20480], P(('parts', 'samp')), parts along dimension 0, may hold values from -6 to 6
- current: bfloat16 [1024, 256], P(('parts', 'samp')), parts along dimension 0, may hold values from -6 to 6
- next_packed: int32 [512, 32], P(('parts', 'samp')), parts along dimension 0, may hold values from -2147483648 to 1789569706, as said below
- covariates: float32 [1024, 64], P(('parts', 'samp')), parts along dimension 0, may hold values from -1 to 1
Outputs:
- scores: float32 [40960, 256], P(('parts', 'samp')), parts along dimension 0
- next_block: bfloat16 [1024, 256], P(('parts', 'samp')), parts along dimension 0
There are 2 independent parts, one for each index of `parts`. A program takes and returns all parts, laid end to end along the dimension named above; each array names one. Nothing has to cross between parts.
Inputs may be any that keep to these rules, and one draw needn't show every extreme that they name: Each word holds the dosages (0, 1 or 2) of 16 consecutive samples of one variant, two bits a sample: sample 16 w + j of variant v in bits 2 j and 2 j + 1 of next_packed[v, w], bit 31 being the sign bit of the int32 word.
All inputs are finite; a program needn't handle non-finite values.
Results may differ from a plain program's by a relative error of at most 0.0004.
Values may be sent and summed in bfloat16 or wider, within the bound.
A program may use at most 64 MiB of HBM per device.

v0:
```python
import jax
import jax.numpy as jnp
from jax import lax
from jax.sharding import PartitionSpec as P


def unpack_words(packed_words):
    shifts = 2 * jnp.arange(16, dtype=jnp.int32)
    fields = jnp.bitwise_and(
        lax.shift_right_logical(packed_words[:, :, None], shifts[None, None, :]), 3
    )
    return fields.reshape(packed_words.shape[0], -1).T.astype(jnp.float32)


def over_samples(left, right):
    return lax.dot_general(
        left, right, (((0,), (0,)), ((), ())), preferred_element_type=jnp.float32
    )


def precise_samples(left, right):
    return lax.dot_general(left, right, (((0,), (0,)), ((), ())), precision=lax.Precision.HIGHEST)


def shards(expression, current, next_packed, covariates):
    group_size = lax.axis_size("samp")
    samples_all = expression.shape[0] * group_size
    scale_factor = float(samples_all) ** (-0.5)
    regrouped = lax.all_to_all(expression, "samp", split_axis=1, concat_axis=0, tiled=True)
    scores = (
        over_samples(regrouped, lax.all_gather(current, "samp", axis=0, tiled=True)) * scale_factor
    )
    packed_words = lax.all_to_all(next_packed, "samp", split_axis=1, concat_axis=0, tiled=True)
    dosage = unpack_words(packed_words)
    local_totals = jnp.sum(dosage, axis=0)
    local_proj = precise_samples(covariates, dosage)
    local_covsum = jnp.sum(covariates, axis=0)
    local_squares = jnp.sum(dosage * dosage, axis=0)
    local_gram = precise_samples(covariates, covariates)
    totals, projected, cov_sums, squares, cov_gram = lax.psum(
        (local_totals, local_proj, local_covsum, local_squares, local_gram), "samp"
    )
    average = totals / samples_all
    loading = projected - cov_sums[:, None] * average[None, :]
    leftover = (
        dosage - average[None, :] - jnp.dot(covariates, loading, precision=lax.Precision.HIGHEST)
    )
    mapped = jnp.dot(cov_gram, loading, precision=lax.Precision.HIGHEST)
    sq_norm = (
        squares
        - samples_all * average * average
        - 2.0 * jnp.sum(loading * loading, axis=0)
        + jnp.sum(loading * mapped, axis=0)
    )
    next_block = (leftover * lax.rsqrt(sq_norm / samples_all + 1e-05)[None, :]).astype(jnp.bfloat16)
    return (scores, next_block)


def solution(mesh):
    in_specs = (
        P(("parts", "samp"), None),
        P(("parts", "samp"), None),
        P(("parts", "samp"), None),
        P(("parts", "samp"), None),
    )
    out_specs = (P(("parts", "samp"), None), P(("parts", "samp"), None))
    return jax.shard_map(shards, mesh=mesh, in_specs=in_specs, out_specs=out_specs, check_vma=False)
```

profile of v0, /device:TPU:0, one launch (start us, length us, event | category | flops | bytes accessed | tf_op | source)
XLA Modules:
  0.0 167.3 jit_solution(882091936499760265)
XLA Ops:
  7.2 1.4 copy.12
  8.5 7.4 %all-to-all-start.1 = ((s32[16,16,2]{0,2,1:T(2,128)}), s32[16,16,2]{0,2,1:T(2,128)S(1)}, u32[]{:S(2)}, u32[]{:S(2)}) async-start(s32[16,16,2]{0,2,1:T(2,128)} %bitcast.2), calls=%async_computation.1 | async-start | bytes 32768 | tf_op jit(solution)/shard_map/all_to_all | solution.py:33
  15.9 2.5 %copy.16 = bf16[4,16,8,1280]{3,2,0,1:T(8,128)(2,1)} copy(bf16[4,16,8,1280]{3,2,1,0:T(8,128)(2,1)} %bitcast.37) | data formatting | bytes 2621440 | tf_op jit(solution)/shard_map/all_to_all | solution.py:29
  18.4 4.0 %all-to-all-done.1 = s32[16,16,2]{0,2,1:T(2,128)S(1)} async-done(((s32[16,16,2]{0,2,1:T(2,128)}), s32[16,16,2]{0,2,1:T(2,128)S(1)}, u32[]{:S(2)}, u32[]{:S(2)}) %all-to-all-start.1) | async-done | bytes 2080 | tf_op jit(solution)/shard_map/all_to_all | solution.py:33
  22.4 0.0 copy-start
  22.4 0.0 copy-start.1
  22.4 3.8 %all-to-all-start = ((bf16[32,16,1280]{2,0,1:T(8,128)(2,1)}), bf16[32,16,1280]{2,0,1:T(8,128)(2,1)S(1)}, u32[]{:S(2)}, u32[]{:S(2)}) async-start(bf16[32,16,1280]{2,0,1:T(8,128)(2,1)} %bitcast.36), calls=%async_computation | async-start | bytes 2621440 | tf_op jit(solution)/shard_map/all_to_all | solution.py:29
  26.3 0.0 all-reduce.3.cloned.1.call-start
  26.4 0.1 shift_right_logical.26
  26.4 0.0 copy-done
  26.5 0.0 copy-done.1
  26.5 38.4 %all_gather.3 = bf16[512,256]{1,0:T(8,128)(2,1)S(1)} all-gather(bf16[32,256]{1,0:T(8,128)(2,1)S(1)} %copy-done.1), channel_id=1, replica_groups=mesh['parts'=2,'samp'=16] {'samp'}, dimensions={0}, use_global_device_ids=true | all-gather | bytes 278528 | tf_op jit(solution)/shard_map/all_gather | solution.py:31
  64.9 0.2 fusion.14
  65.1 0.1 shift_right_logical.22
  65.2 0.1 fusion.9
  65.3 0.1 fusion.5
  65.4 0.9 convolution_bitcast_fusion
  66.2 0.0 all-reduce.3.cloned.1.call-update
  66.3 63.2 %all-reduce = (f32[256]{0:T(256)S(1)}, f32[64]{0:T(128)S(1)}, f32[64,64]{1,0:T(8,128)S(1)}, f32[256]{0:T(256)S(1)}) all-reduce(f32[256]{0:T(256)S(1)} %get-tuple-element.3, f32[64]{0:T(128)S(1)} %reduce_sum.46, f32[64,64]{1,0:T(8,128)S(1)} %fusion.14, f32[256]{0:T(256)S(1)} %get-tuple-element.2), channel_id=1, replica_groups=mesh['parts'=2,'samp'=16] {'samp'}, use_global_device_ids=true, to_apply=%region_1.0 | all-reduce | flops 4672 | bytes 37376 | tf_op jit(solution)/shard_map/psum | solution.py:40
  129.4 0.1 fusion.7
  129.5 25.5 %all-reduce.3.cloned.1.call-done = f32[64,256]{1,0:T(8,128)} async-done(((f32[64,256]{1,0:T(8,128)}), f32[64,256]{1,0:T(8,128)}) %all-reduce.3.cloned.1.call-update) | async-done | bytes 65552 | tf_op jit(solution)/shard_map/psum | solution.py:40
  155.1 0.9 multiply_reduce_fusion
  156.0 1.1 fusion
  157.1 1.7 %fusion.3 = bf16[32,256]{1,0:T(8,128)(2,1)} fusion(f32[256,32]{0,1:T(8,128)S(1)} %fusion.7, f32[32,64]{1,0:T(8,128)S(1)} %copy-done, f32[64,256]{1,0:T(8,128)} %all-reduce.3.cloned.1.call-done, f32[256]{0:T(256)S(1)} %broadcast_multiply_fusion, f32[64]{0:T(128)S(1)} %get-tuple-element.5, f32[256]{0:T(256)S(1)} %add_rsqrt_fusion), kind=kOutput, calls=%fused_computation.8 | convolution fusion | flops 6348800 | bytes 125184 | tf_op jit(solution)/shard_map/dot_general | solution.py:46
  158.8 0.0 all-to-all-done
  158.8 1.6 convolution_multiply_fusion
  (6 shorter events, 0.0 us)
Async XLA Ops:
  8.5 13.9 %all-to-all-start.1 = ((s32[16,16,2]{0,2,1:T(2,128)}), s32[16,16,2]{0,2,1:T(2,128)S(1)}, u32[]{:S(2)}, u32[]{:S(2)}) async-start(s32[16,16,2]{0,2,1:T(2,128)} %bitcast.2), calls=%async_computation.1 | async-start | bytes 32768 | tf_op jit(solution)/shard_map/all_to_all | solution.py:33
  22.4 4.0 %copy-start = (f32[32,64]{1,0:T(8,128)S(1)}, f32[32,64]{1,0:T(8,128)}, u32[]{:S(2)}) copy-start(f32[32,64]{1,0:T(8,128)} %param.7) | copy-start | bytes 24580
  22.4 4.0 %copy-start.1 = (bf16[32,256]{1,0:T(8,128)(2,1)S(1)}, bf16[32,256]{1,0:T(8,128)(2,1)}, u32[]{:S(2)}) copy-start(bf16[32,256]{1,0:T(8,128)(2,1)} %param.5) | copy-start | bytes 49156
  22.4 136.4 %all-to-all-start = ((bf16[32,16,1280]{2,0,1:T(8,128)(2,1)}), bf16[32,16,1280]{2,0,1:T(8,128)(2,1)S(1)}, u32[]{:S(2)}, u32[]{:S(2)}) async-start(bf16[32,16,1280]{2,0,1:T(8,128)(2,1)} %bitcast.36), calls=%async_computation | async-start | bytes 2621440 | tf_op jit(solution)/shard_map/all_to_all | solution.py:29
  26.3 128.8 %all-reduce.3.cloned.1.call-start = ((), (), s32[]{:S(2)}) async-start(), calls=%async_computation.2 | async-start | bytes 131072 | tf_op jit(solution)/shard_map/psum | solution.py:40
Sparse Core Ops, SparseCore 0:
  66.4 88.6 all-reduce.2
where the time goes:
time: 169 us; the launch traced here: 167 us
  blocking collectives  102 us (60%)
  waiting for transfers between devices  29.5 us (17%)
  between operations  14.1 us (8%)
  starting transfers between devices  11.3 us (7%)
  matrix products  5.53 us (3%)
  local copies, waits for them, and re-layouts  4.06 us (2%)
    psum x1, blocking collectives, shards(): lax.psum((local_totals, local_proj, local_covsum, local_squares, local_gr...  63.2 us
    all_gather x1, blocking collectives, shards(): lax.all_gather(current, 'samp', axis=0, tiled=True)  38.4 us
    psum x1, waiting for transfers between devices, shards(): lax.psum((local_totals, local_proj, local_covsum, local_squares, local_gr...  25.5 us
    all_to_all x1, starting transfers between devices, shards(): lax.all_to_all(next_packed, 'samp', split_axis=1, concat_axis=0, tiled=True)  7.39 us
    all_to_all x1, waiting for transfers between devices, shards(): lax.all_to_all(next_packed, 'samp', split_axis=1, concat_axis=0, tiled=True)  3.99 us
    all_to_all x1, starting transfers between devices, shards(): lax.all_to_all(expression, 'samp', split_axis=1, concat_axis=0, tiled=True)  3.83 us
  transfers between devices with their start and end apart: 3, of which 2 were waited for; matrix products, arithmetic and copies ran while one was open for 5% of the time, Pallas kernels for 0%

commit v1 on v0

--- a/solution.py
+++ b/solution.py
@@ -1,7 +1,14 @@
+import functools
+
 import jax
 import jax.numpy as jnp
 from jax import lax
+from jax.experimental import pallas as pl
+from jax.experimental.pallas import tpu as pltpu
 from jax.sharding import PartitionSpec as P
+
+MESH = pl.DeviceIdType.MESH
+CORES = 2
 
 
 def unpack_words(packed_words):
@@ -22,7 +29,238 @@
     return lax.dot_general(left, right, (((0,), (0,)), ((), ())), precision=lax.Precision.HIGHEST)
 
 
+def grid_of(group_size):
+    chips = group_size // CORES
+    across = 2 ** ((chips.bit_length() - 1) // 3)
+    return chips // across, across
+
+
+def exchange_kernel(
+    depth,
+    across,
+    genes,
+    expr_ref,
+    current_ref,
+    packed_ref,
+    cov_ref,
+    tiles_ref,
+    current_all,
+    next_ref,
+    cov_all,
+    packed_all,
+    dosage_ref,
+    words_ref,
+    own_sem,
+    bulk_send,
+    bulk_recv,
+    small_send,
+    small_recv,
+):
+    me = lax.axis_index("samp")
+    core = lax.rem(me, CORES)
+    column = lax.rem(me // CORES, across)
+    level = me // (CORES * across)
+    group_size = CORES * across * depth
+    rows = cov_ref.shape[0]
+    inward = jnp.where(level < depth // 2, 1, depth - 1)
+
+    def member(dz, dx, dc):
+        z = lax.rem(level + inward * dz, depth)
+        x = lax.rem(column + dx, across)
+        c = lax.rem(core + dc, CORES)
+        return (z * across + x) * CORES + c
+
+    barrier = pltpu.get_barrier_semaphore()
+    for step in range(1, group_size):
+        pl.semaphore_signal(
+            barrier,
+            inc=1,
+            device_id={"samp": lax.rem(me + step, group_size)},
+            device_id_type=MESH,
+        )
+    pl.semaphore_wait(barrier, group_size - 1)
+
+    small = ((current_ref, current_all), (packed_ref, packed_all), (cov_ref, cov_all))
+    own_copies = []
+    for k, (own, whole) in enumerate(small):
+        own_copies.append(
+            pltpu.make_async_copy(own, whole.at[level, column, core], own_sem.at[k])
+        )
+    mine = pl.ds(pl.multiple_of(me * genes, 128), genes)
+    own_copies.append(
+        pltpu.make_async_copy(expr_ref.at[:, mine], tiles_ref.at[me], own_sem.at[len(small)])
+    )
+    for copy in own_copies:
+        copy.start()
+
+    def small_along_z(k, dz, sender_level):
+        own, whole = small[k]
+        target = (lax.rem(level + dz, depth) * across + column) * CORES + core
+        return pltpu.make_async_remote_copy(
+            src_ref=own,
+            dst_ref=whole.at[sender_level, column, core],
+            send_sem=small_send.at[k, dz],
+            recv_sem=small_recv.at[k, dz],
+            device_id={"samp": target},
+            device_id_type=MESH,
+        )
+
+    def bulk(other, sender):
+        span = pl.ds(pl.multiple_of(other * genes, 128), genes)
+        return pltpu.make_async_remote_copy(
+            src_ref=expr_ref.at[:, span],
+            dst_ref=tiles_ref.at[sender],
+            send_sem=bulk_send.at[other],
+            recv_sem=bulk_recv.at[sender],
+            device_id={"samp": other},
+            device_id_type=MESH,
+        )
+
+    for dz in range(1, depth):
+        for k in range(len(small)):
+            small_along_z(k, dz, level).start()
+    same_column = [(dz, 0, dc) for dz in range(1, depth) for dc in range(CORES)]
+    others = [
+        (dz, dx, dc)
+        for dz in [*range(1, depth), 0]
+        for dx in range(1, across)
+        for dc in range(CORES)
+    ]
+    for offset in same_column:
+        bulk(member(*offset), me).start()
+    for copy in own_copies[: len(small)]:
+        copy.wait()
+    for dz in range(1, depth):
+        for k in range(len(small)):
+            small_along_z(k, dz, lax.rem(level - dz + depth, depth)).wait_recv()
+
+    def small_along_x(k, dx, sender_column):
+        whole = small[k][1]
+        target = (level * across + lax.rem(column + dx, across)) * CORES + core
+        return pltpu.make_async_remote_copy(
+            src_ref=whole.at[:, column, core],
+            dst_ref=whole.at[:, sender_column, core],
+            send_sem=small_send.at[k, depth + dx],
+            recv_sem=small_recv.at[k, depth + dx],
+            device_id={"samp": target},
+            device_id_type=MESH,
+        )
+
+    for dx in range(1, across):
+        for k in range(len(small)):
+            small_along_x(k, dx, column).start()
+    for offset in others:
+        bulk(member(*offset), me).start()
+    bulk(member(0, 0, 1), me).start()
+    for dx in range(1, across):
+        for k in range(len(small)):
+            small_along_x(k, dx, lax.rem(column - dx + across, across)).wait_recv()
+
+    def small_to_core(k, sender_core):
+        whole = small[k][1]
+        return pltpu.make_async_remote_copy(
+            src_ref=whole.at[:, :, core],
+            dst_ref=whole.at[:, :, sender_core],
+            send_sem=small_send.at[k, 0],
+            recv_sem=small_recv.at[k, 0],
+            device_id={"samp": me - core + (1 - core)},
+            device_id_type=MESH,
+        )
+
+    for k in range(len(small)):
+        small_to_core(k, core).start()
+    for k in range(len(small)):
+        small_to_core(k, 1 - core).wait_recv()
+
+    samples = group_size * rows
+    variants = group_size * packed_ref.shape[0]
+    word_count = packed_ref.shape[1]
+    words_ref[...] = packed_all[...].reshape(variants, word_count).T
+    shifts = 2 * lax.broadcasted_iota(jnp.int32, (16, variants), 0)
+
+    @pl.loop(0, word_count)
+    def _(word):
+        held = jnp.broadcast_to(words_ref[pl.ds(word, 1), :], (16, variants))
+        fields = jnp.bitwise_and(lax.shift_right_logical(held, shifts), 3)
+        dosage_ref[pl.ds(pl.multiple_of(word * 16, 16), 16), :] = fields.astype(jnp.float32)
+
+    cov = cov_all[...].reshape(samples, cov_ref.shape[1])
+    average = jnp.sum(dosage_ref[...], axis=0, keepdims=True) / samples
+    projected = precise_samples(cov, dosage_ref[...])
+    cov_sums = precise_samples(cov, jnp.ones((samples, 128), jnp.float32))[:, :1]
+    loading = projected - cov_sums * average
+    leftover = (
+        dosage_ref[...]
+        - average
+        - jnp.dot(cov, loading, precision=lax.Precision.HIGHEST, preferred_element_type=jnp.float32)
+    )
+    sq_norm = jnp.sum(leftover * leftover, axis=0, keepdims=True)
+    dosage_ref[...] = leftover
+    here = dosage_ref[pl.ds(pl.multiple_of(me * rows, 8), rows), :]
+    next_ref[...] = (here * lax.rsqrt(sq_norm / samples + 1e-05)).astype(next_ref.dtype)
+
+    own_copies[-1].wait()
+    for offset in [*same_column, *others, (0, 0, 1)]:
+        other = member(*offset)
+        bulk(other, me).wait_send()
+    for step in range(1, group_size):
+        bulk(me, lax.rem(me + step, group_size)).wait_recv()
+    for k in range(len(small)):
+        for dz in range(1, depth):
+            small_along_z(k, dz, level).wait_send()
+        for dx in range(1, across):
+            small_along_x(k, dx, column).wait_send()
+        small_to_core(k, core).wait_send()
+
+
+def exchange(expression, current, next_packed, covariates, group_size):
+    depth, across = grid_of(group_size)
+    rows, all_genes = expression.shape
+    genes = all_genes // group_size
+    variants = next_packed.shape[0] * group_size
+    lead = (depth, across, CORES)
+    vmem = pl.BlockSpec(memory_space=pltpu.VMEM)
+    hbm = pl.BlockSpec(memory_space=pl.ANY)
+    return pl.pallas_call(
+        functools.partial(exchange_kernel, depth, across, genes),
+        out_shape=(
+            jax.ShapeDtypeStruct((group_size, rows, genes), expression.dtype),
+            jax.ShapeDtypeStruct((*lead, *current.shape), current.dtype),
+            jax.ShapeDtypeStruct(current.shape, jnp.bfloat16),
+        ),
+        in_specs=[hbm, vmem, vmem, vmem],
+        out_specs=(hbm, vmem, vmem),
+        scratch_shapes=[
+            pltpu.VMEM((*lead, *covariates.shape), covariates.dtype),
+            pltpu.VMEM((*lead, *next_packed.shape), next_packed.dtype),
+            pltpu.VMEM((rows * group_size, variants), jnp.float32),
+            pltpu.VMEM((next_packed.shape[1], variants), jnp.int32),
+            pltpu.SemaphoreType.DMA((4,)),
+            pltpu.SemaphoreType.DMA((group_size,)),
+            pltpu.SemaphoreType.DMA((group_size,)),
+            pltpu.SemaphoreType.DMA((3, depth + across)),
+            pltpu.SemaphoreType.DMA((3, depth + across)),
+        ],
+        compiler_params=pltpu.CompilerParams(collective_id=0, has_side_effects=True),
+    )(expression, current, next_packed, covariates)
+
+
 def shards(expression, current, next_packed, covariates):
+    group_size = lax.axis_size("samp")
+    samples_all = expression.shape[0] * group_size
+    scale_factor = float(samples_all) ** (-0.5)
+    genes = expression.shape[1] // group_size
+    if genes % 128 == 0 and next_packed.shape[0] % 8 == 0:
+        tiles, current_all, next_block = exchange(
+            expression, current, next_packed, covariates, group_size
+        )
+        regrouped = tiles.reshape(samples_all, genes)
+        everyone = current_all.reshape(samples_all, current.shape[1])
+        return (over_samples(regrouped, everyone) * scale_factor, next_block)
+    return shards_by_xla(expression, current, next_packed, covariates)
+
+
+def shards_by_xla(expression, current, next_packed, covariates):
     group_size = lax.axis_size("samp")
     samples_all = expression.shape[0] * group_size
     scale_factor = float(samples_all) ** (-0.5)

time: 169 us -> 45.9 us (0.27)
  blocking collectives: 102 us -> 0 us
  Pallas kernels: 0 us -> 41.4 us
  waiting for transfers between devices: 29.5 us -> 0 us
  between operations: 14.1 us -> 0.65 us
  starting transfers between devices: 11.3 us -> 0 us
  local copies, waits for them, and re-layouts: 4.06 us -> 0.61 us
  matrix products: 5.53 us -> 2.95 us
    psum x1 -> x0, blocking collectives: 63.2 us -> none  [shards(): lax.psum((local_totals, local_proj, local_covsum, local_squares, local_gr...]
    pallas_call x0 -> x1, Pallas kernels: none -> 41.4 us  [exchange(): pl.pallas_call(functools.partial(exchange_kernel, depth, across, genes),...]
    all_gather x1 -> x0, blocking collectives: 38.4 us -> none  [shards(): lax.all_gather(current, 'samp', axis=0, tiled=True)]
    psum x1 -> x0, waiting for transfers between devices: 25.5 us -> none  [shards(): lax.psum((local_totals, local_proj, local_covsum, local_squares, local_gr...]
    all_to_all x2 -> x0, starting transfers between devices: 11.2 us -> none  [the longest x1 7.39 us: shards(): lax.all_to_all(next_packed, 'samp', split_axis=1, concat_axis=0, tiled=True)]
    all_to_all x2 -> x0, waiting for transfers between devices: 4 us -> none  [the longest x1 3.99 us: shards(): lax.all_to_all(next_packed, 'samp', split_axis=1, concat_axis=0, tiled=True)]
    dot_general x4 -> x0, matrix products: 3.92 us -> none  [the longest x1 1.69 us: shards(): jnp.dot(covariates, loading, precision=lax.Precision.HIGHEST)]
    all_to_all x2 -> x0, local copies, waits for them, and re-layouts: 2.51 us -> none  [the longest x1 2.51 us: shards(): lax.all_to_all(expression, 'samp', split_axis=1, concat_axis=0, tiled=True)]
  transfers between devices with their start and end apart: 3 -> 0, of which waited for: 2 -> 0; matrix products, arithmetic and copies ran while one was open for 5% -> 0% of each run, Pallas kernels for 0% -> 0%
where the time goes in v1:
time: 45.9 us; the launch traced here: 45.6 us
  Pallas kernels  41.4 us (90%)
  matrix products  2.95 us (6%)
  between operations  0.65 us (1%)
  local copies, waits for them, and re-layouts  0.61 us (1%)
    pallas_call x1, Pallas kernels, exchange(): pl.pallas_call(functools.partial(exchange_kernel, depth, across, genes),...  41.4 us
    dot_general x1, matrix products, over_samples(): lax.dot_general(left, right, (((0,), (0,)), ((), ())), preferred_element_...  2.95 us

profile of v1, /device:TPU:0, one launch (start us, length us, event | category | flops | bytes accessed | tf_op | source)
XLA Modules:
  0.0 45.6 jit_solution(9302829786494045297)
XLA Ops:
  0.6 41.4 %shard_map.59 = (bf16[16,32,1280]{2,1,0:T(8,128)(2,1)}, bf16[4,2,2,32,256]{4,3,2,1,0:T(8,128)(2,1)}, bf16[32,256]{1,0:T(8,128)(2,1)}) custom-call(bf16[32,20480]{1,0:T(8,128)(2,1)} %expr_ref.1, bf16[32,256]{1,0:T(8,128)(2,1)} %current_ref.1, s32[16,32]{1,0:T(8,128)} %packed_ref.1, f32[32,64]{1,0:T(8,128)} %cov_ref.1), custom_call_target="tpu_custom_call" | custom-call | tf_op jit(solution)/shard_map/pallas_call | solution.py:224
  42.1 0.0 copy-start
  42.1 3.0 %convolution_multiply_fusion = f32[1280,256]{1,0:T(8,128)} fusion(bf16[512,1280]{1,0:T(8,128)(2,1)} %bitcast.4, bf16[512,256]{1,0:T(8,128)(2,1)} %bitcast.5), kind=kOutput, calls=%fused_computation | convolution fusion | flops 335872000 | bytes 2883584 | tf_op jit(solution)/shard_map/dot_general | solution.py:23
  45.0 0.0 copy-done
  45.0 0.6 %copy.7 = bf16[32,256]{1,0:T(8,128)(2,1)} copy(bf16[32,256]{1,0:T(8,128)(2,1)S(1)} %copy-done) | data formatting | bytes 32768
Async XLA Ops:
  42.1 3.0 %copy-start = (bf16[32,256]{1,0:T(8,128)(2,1)S(1)}, bf16[32,256]{1,0:T(8,128)(2,1)}, u32[]{:S(2)}) copy-start(bf16[32,256]{1,0:T(8,128)(2,1)} %get-tuple-element.11) | copy-start | bytes 49156

commit v2 on v1

--- a/solution.py
+++ b/solution.py
@@ -55,6 +55,9 @@
     bulk_recv,
     small_send,
     small_recv,
+    row_send,
+    row_recv,
+    ready_sem,
 ):
     me = lax.axis_index("samp")
     core = lax.rem(me, CORES)
@@ -62,46 +65,95 @@
     level = me // (CORES * across)
     group_size = CORES * across * depth
     rows = cov_ref.shape[0]
-    inward = jnp.where(level < depth // 2, 1, depth - 1)
-
-    def member(dz, dx, dc):
-        z = lax.rem(level + inward * dz, depth)
-        x = lax.rem(column + dx, across)
-        c = lax.rem(core + dc, CORES)
+    last = depth - 1
+
+    def at(z, x, c):
         return (z * across + x) * CORES + c
 
-    barrier = pltpu.get_barrier_semaphore()
-    for step in range(1, group_size):
-        pl.semaphore_signal(
-            barrier,
-            inc=1,
-            device_id={"samp": lax.rem(me + step, group_size)},
+    def on_line(dz, act):
+        z = level + dz
+        pl.when(jnp.logical_and(z >= 0, z <= last))(functools.partial(act, z))
+
+    row_mates = [
+        (dx, dc) for dx in range(across) for dc in range(CORES) if (dx, dc) != (0, 0)
+    ]
+
+    def row_mate(z, dx, dc):
+        return at(z, lax.rem(column + dx, across), lax.rem(core + dc, CORES))
+
+    near_count = len(row_mates) + CORES * (
+        jnp.where(level > 0, 1, 0) + jnp.where(level < last, 1, 0)
+    )
+
+    def greet(sem):
+        def tell(target):
+            pl.semaphore_signal(sem, inc=1, device_id={"samp": target}, device_id_type=MESH)
+
+        def both_cores(z):
+            for dc in range(CORES):
+                tell(row_mate(z, 0, dc))
+
+        on_line(1, both_cores)
+        on_line(-1, both_cores)
+        for dx, dc in row_mates:
+            tell(row_mate(level, dx, dc))
+
+    small = ((current_ref, current_all), (packed_ref, packed_all), (cov_ref, cov_all))
+
+    def small_on_line(k, hop, step, source):
+        own, whole = small[k]
+        return pltpu.make_async_remote_copy(
+            src_ref=own if hop == 0 else whole.at[source, column, core],
+            dst_ref=whole.at[source, column, core],
+            send_sem=small_send.at[k, hop * 2 + (step + 1) // 2],
+            recv_sem=small_recv.at[k, source],
+            device_id={"samp": at(level + step, column, core)},
             device_id_type=MESH,
         )
-    pl.semaphore_wait(barrier, group_size - 1)
-
-    small = ((current_ref, current_all), (packed_ref, packed_all), (cov_ref, cov_all))
-    own_copies = []
-    for k, (own, whole) in enumerate(small):
-        own_copies.append(
-            pltpu.make_async_copy(own, whole.at[level, column, core], own_sem.at[k])
-        )
-    mine = pl.ds(pl.multiple_of(me * genes, 128), genes)
-    own_copies.append(
-        pltpu.make_async_copy(expr_ref.at[:, mine], tiles_ref.at[me], own_sem.at[len(small)])
-    )
-    for copy in own_copies:
-        copy.start()
-
-    def small_along_z(k, dz, sender_level):
-        own, whole = small[k]
-        target = (lax.rem(level + dz, depth) * across + column) * CORES + core
+
+    def relay(hop, step, finish):
+        source = level - hop * step
+        goes = jnp.logical_and(
+            jnp.logical_and(source >= 0, source <= last),
+            jnp.logical_and(level + step >= 0, level + step <= last),
+        )
+
+        @pl.when(goes)
+        def _():
+            for k in range(len(small)):
+                copy = small_on_line(k, hop, step, source)
+                if finish:
+                    copy.wait_send()
+                else:
+                    copy.start()
+
+    def arrive(distance):
+        def take(z):
+            for k in range(len(small)):
+                small_on_line(k, 1, 1, z).wait_recv()
+
+        on_line(distance, take)
+        on_line(-distance, take)
+
+    def small_on_row(k, dx, sender_column):
+        whole = small[k][1]
         return pltpu.make_async_remote_copy(
-            src_ref=own,
-            dst_ref=whole.at[sender_level, column, core],
-            send_sem=small_send.at[k, dz],
-            recv_sem=small_recv.at[k, dz],
-            device_id={"samp": target},
+            src_ref=whole.at[:, column, core],
+            dst_ref=whole.at[:, sender_column, core],
+            send_sem=row_send.at[k, dx],
+            recv_sem=row_recv.at[k, dx],
+            device_id={"samp": at(level, lax.rem(column + dx, across), core)},
+            device_id_type=MESH,
+        )
+
+    def small_to_core(k, sender_core):
+        whole = small[k][1]
+        return pltpu.make_async_remote_copy(
+            src_ref=whole.at[:, :, core],
+            dst_ref=whole.at[:, :, sender_core],
+            send_sem=row_send.at[k, 0],
+            recv_sem=row_recv.at[k, 0],
+            device_id={"samp": at(level, column, 1 - core)},
             device_id_type=MESH,
         )
 
@@ -116,57 +168,62 @@
             device_id_type=MESH,
         )
 
-    for dz in range(1, depth):
-        for k in range(len(small)):
-            small_along_z(k, dz, level).start()
-    same_column = [(dz, 0, dc) for dz in range(1, depth) for dc in range(CORES)]
-    others = [
-        (dz, dx, dc)
-        for dz in [*range(1, depth), 0]
-        for dx in range(1, across)
-        for dc in range(CORES)
-    ]
-    for offset in same_column:
-        bulk(member(*offset), me).start()
+    def send_tiles(dz, columns):
+        def start(z):
+            for dx in columns:
+                for dc in range(CORES):
+                    bulk(row_mate(z, dx, dc), me).start()
+
+        on_line(dz, start)
+        on_line(-dz, start)
+
+    barrier = pltpu.get_barrier_semaphore()
+    greet(barrier)
+    own_copies = []
+    for k, (own, whole) in enumerate(small):
+        own_copies.append(
+            pltpu.make_async_copy(own, whole.at[level, column, core], own_sem.at[k])
+        )
+    mine = pl.ds(pl.multiple_of(me * genes, 128), genes)
+    own_copies.append(
+        pltpu.make_async_copy(expr_ref.at[:, mine], tiles_ref.at[me], own_sem.at[len(small)])
+    )
+    for copy in own_copies:
+        copy.start()
+    pl.semaphore_wait(barrier, near_count)
+
+    elsewhere = list(range(1, across))
+    for hops in range(1, depth + 1):
+        if hops < depth:
+            greet(ready_sem.at[hops - 1])
+        if hops == 1:
+            relay(0, 1, False)
+            relay(0, -1, False)
+        if hops == 2:
+            arrive(1)
+            relay(1, 1, False)
+            relay(1, -1, False)
+        if hops < depth:
+            send_tiles(hops, [0])
+        if hops >= 2:
+            send_tiles(hops - 1, elsewhere)
+        if hops < depth:
+            pl.semaphore_wait(ready_sem.at[hops - 1], near_count)
+    for dx, dc in row_mates:
+        bulk(row_mate(level, dx, dc), me).start()
+    for distance in range(2, depth):
+        arrive(distance)
+        if distance < last:
+            relay(distance, 1, False)
+            relay(distance, -1, False)
     for copy in own_copies[: len(small)]:
         copy.wait()
-    for dz in range(1, depth):
+    for dx in elsewhere:
         for k in range(len(small)):
-            small_along_z(k, dz, lax.rem(level - dz + depth, depth)).wait_recv()
-
-    def small_along_x(k, dx, sender_column):
-        whole = small[k][1]
-        target = (level * across + lax.rem(column + dx, across)) * CORES + core
-        return pltpu.make_async_remote_copy(
-            src_ref=whole.at[:, column, core],
-            dst_ref=whole.at[:, sender_column, core],
-            send_sem=small_send.at[k, depth + dx],
-            recv_sem=small_recv.at[k, depth + dx],
-            device_id={"samp": target},
-            device_id_type=MESH,
-        )
-
-    for dx in range(1, across):
+            small_on_row(k, dx, column).start()
+    for dx in elsewhere:
         for k in range(len(small)):
-            small_along_x(k, dx, column).start()
-    for offset in others:
-        bulk(member(*offset), me).start()
-    bulk(member(0, 0, 1), me).start()
-    for dx in range(1, across):
-        for k in range(len(small)):
-            small_along_x(k, dx, lax.rem(column - dx + across, across)).wait_recv()
-
-    def small_to_core(k, sender_core):
-        whole = small[k][1]
-        return pltpu.make_async_remote_copy(
-            src_ref=whole.at[:, :, core],
-            dst_ref=whole.at[:, :, sender_core],
-            send_sem=small_send.at[k, 0],
-            recv_sem=small_recv.at[k, 0],
-            device_id={"samp": me - core + (1 - core)},
-            device_id_type=MESH,
-        )
-
+            small_on_row(k, dx, lax.rem(column - dx + across, across)).wait_recv()
     for k in range(len(small)):
         small_to_core(k, core).start()
     for k in range(len(small)):
@@ -200,16 +257,16 @@
     next_ref[...] = (here * lax.rsqrt(sq_norm / samples + 1e-05)).astype(next_ref.dtype)
 
     own_copies[-1].wait()
-    for offset in [*same_column, *others, (0, 0, 1)]:
-        other = member(*offset)
-        bulk(other, me).wait_send()
+    for step in range(1, group_size):
+        bulk(lax.rem(me + step, group_size), me).wait_send()
     for step in range(1, group_size):
         bulk(me, lax.rem(me + step, group_size)).wait_recv()
+    for hop in range(last):
+        relay(hop, 1, True)
+        relay(hop, -1, True)
     for k in range(len(small)):
-        for dz in range(1, depth):
-            small_along_z(k, dz, level).wait_send()
-        for dx in range(1, across):
-            small_along_x(k, dx, column).wait_send()
+        for dx in elsewhere:
+            small_on_row(k, dx, column).wait_send()
         small_to_core(k, core).wait_send()
 
 
@@ -220,7 +277,8 @@
     variants = next_packed.shape[0] * group_size
     lead = (depth, across, CORES)
     vmem = pl.BlockSpec(memory_space=pltpu.VMEM)
-    hbm = pl.BlockSpec(memory_space=pl.ANY)
+    hbm = pl.BlockSpec(memory_space=pltpu.HBM)
+    anywhere = pl.BlockSpec(memory_space=pl.ANY)
     return pl.pallas_call(
         functools.partial(exchange_kernel, depth, across, genes),
         out_shape=(
@@ -228,8 +286,8 @@
             jax.ShapeDtypeStruct((*lead, *current.shape), current.dtype),
             jax.ShapeDtypeStruct(current.shape, jnp.bfloat16),
         ),
-        in_specs=[hbm, vmem, vmem, vmem],
-        out_specs=(hbm, vmem, vmem),
+        in_specs=[hbm] * 4,
+        out_specs=(anywhere, vmem, vmem),
         scratch_shapes=[
             pltpu.VMEM((*lead, *covariates.shape), covariates.dtype),
             pltpu.VMEM((*lead, *next_packed.shape), next_packed.dtype),
@@ -238,10 +296,15 @@
             pltpu.SemaphoreType.DMA((4,)),
             pltpu.SemaphoreType.DMA((group_size,)),
             pltpu.SemaphoreType.DMA((group_size,)),
-            pltpu.SemaphoreType.DMA((3, depth + across)),
-            pltpu.SemaphoreType.DMA((3, depth + across)),
+            pltpu.SemaphoreType.DMA((3, 2 * depth)),
+            pltpu.SemaphoreType.DMA((3, depth)),
+            pltpu.SemaphoreType.DMA((3, across)),
+            pltpu.SemaphoreType.DMA((3, across)),
+            pltpu.SemaphoreType.REGULAR((depth,)),
         ],
-        compiler_params=pltpu.CompilerParams(collective_id=0, has_side_effects=True),
+        compiler_params=pltpu.CompilerParams(
+            collective_id=0, has_side_effects=True
+        ),
     )(expression, current, next_packed, covariates)
 
 

time: 45.9 us -> 43.2 us (0.941)
  Pallas kernels: 41.4 us -> 38.8 us
    pallas_call x1, Pallas kernels: 41.4 us -> 38.8 us  [exchange(): pl.pallas_call(functools.partial(exchange_kernel, depth, across, genes),...]
where the time goes in v2:
time: 43.2 us; the launch traced here: 43 us
  Pallas kernels  38.8 us (90%)
  matrix products  2.95 us (7%)
  between operations  0.65 us (2%)
  local copies, waits for them, and re-layouts  0.61 us (1%)
    pallas_call x1, Pallas kernels, exchange(): pl.pallas_call(functools.partial(exchange_kernel, depth, across, genes),...  38.8 us
    dot_general x1, matrix products, over_samples(): lax.dot_general(left, right, (((0,), (0,)), ((), ())), preferred_element_...  2.95 us

profile of v2, /device:TPU:0, one launch (start us, length us, event | category | flops | bytes accessed | tf_op | source)
XLA Modules:
  0.0 43.0 jit_solution(7690303598138043722)
XLA Ops:
  0.6 38.8 %shard_map.59 = (bf16[16,32,1280]{2,1,0:T(8,128)(2,1)}, bf16[4,2,2,32,256]{4,3,2,1,0:T(8,128)(2,1)}, bf16[32,256]{1,0:T(8,128)(2,1)}) custom-call(bf16[32,20480]{1,0:T(8,128)(2,1)} %expr_ref.1, bf16[32,256]{1,0:T(8,128)(2,1)} %current_ref.1, s32[16,32]{1,0:T(8,128)} %packed_ref.1, f32[32,64]{1,0:T(8,128)} %cov_ref.1), custom_call_target="tpu_custom_call" | custom-call | tf_op jit(solution)/shard_map/pallas_call | solution.py:282
  39.4 0.0 copy-start
  39.5 3.0 %convolution_multiply_fusion = f32[1280,256]{1,0:T(8,128)} fusion(bf16[512,1280]{1,0:T(8,128)(2,1)} %bitcast.4, bf16[512,256]{1,0:T(8,128)(2,1)} %bitcast.5), kind=kOutput, calls=%fused_computation | convolution fusion | flops 335872000 | bytes 2883584 | tf_op jit(solution)/shard_map/dot_general | solution.py:23
  42.4 0.0 copy-done
  42.4 0.6 %copy.7 = bf16[32,256]{1,0:T(8,128)(2,1)} copy(bf16[32,256]{1,0:T(8,128)(2,1)S(1)} %copy-done) | data formatting | bytes 32768
Async XLA Ops:
  39.4 3.0 %copy-start = (bf16[32,256]{1,0:T(8,128)(2,1)S(1)}, bf16[32,256]{1,0:T(8,128)(2,1)}, u32[]{:S(2)}) copy-start(bf16[32,256]{1,0:T(8,128)(2,1)} %get-tuple-element.11) | copy-start | bytes 49156

commit v3 on v2

--- a/solution.py
+++ b/solution.py
@@ -308,6 +308,37 @@
     )(expression, current, next_packed, covariates)
 
 
+def scores_kernel(scale_factor, tiles_ref, current_ref, carried_ref, scores_ref, next_ref):
+    scores_ref[...] = over_samples(tiles_ref[...], current_ref[...]) * scale_factor
+
+    @pl.when(pl.program_id(0) == 0)
+    def _():
+        next_ref[...] = carried_ref[...]
+
+
+def score(regrouped, everyone, next_block, scale_factor):
+    samples, genes = regrouped.shape
+    variants = everyone.shape[1]
+    width = genes // 2 if genes % 256 == 0 else 128
+    return pl.pallas_call(
+        functools.partial(scores_kernel, scale_factor),
+        grid=(genes // width,),
+        out_shape=(
+            jax.ShapeDtypeStruct((genes, variants), jnp.float32),
+            jax.ShapeDtypeStruct(next_block.shape, next_block.dtype),
+        ),
+        in_specs=[
+            pl.BlockSpec((samples, width), lambda i: (0, i)),
+            pl.BlockSpec(everyone.shape, lambda i: (0, 0)),
+            pl.BlockSpec(next_block.shape, lambda i: (0, 0)),
+        ],
+        out_specs=(
+            pl.BlockSpec((width, variants), lambda i: (i, 0)),
+            pl.BlockSpec(next_block.shape, lambda i: (0, 0)),
+        ),
+    )(regrouped, everyone, next_block)
+
+
 def shards(expression, current, next_packed, covariates):
     group_size = lax.axis_size("samp")
     samples_all = expression.shape[0] * group_size
@@ -319,7 +350,7 @@
         )
         regrouped = tiles.reshape(samples_all, genes)
         everyone = current_all.reshape(samples_all, current.shape[1])
-        return (over_samples(regrouped, everyone) * scale_factor, next_block)
+        return tuple(score(regrouped, everyone, next_block, scale_factor))
     return shards_by_xla(expression, current, next_packed, covariates)
 
 

time: 43.2 us -> 42.4 us (0.981)
  matrix products: 2.95 us -> 0 us
  Pallas kernels: 38.8 us -> 41.6 us
  local copies, waits for them, and re-layouts: 0.61 us -> 0 us
    dot_general x1 -> x0, matrix products: 2.95 us -> none  [over_samples(): lax.dot_general(left, right, (((0,), (0,)), ((), ())), preferred_element_...]
    pallas_call x0 -> x1, Pallas kernels: none -> 2.82 us  [score(): pl.pallas_call(functools.partial(scores_kernel, scale_factor), grid=(gene...]
    unnamed x3 -> x0, local copies, waits for them, and re-layouts: 0.61 us -> none
where the time goes in v3:
time: 42.4 us; the launch traced here: 42.3 us
  Pallas kernels  41.6 us (98%)
  between operations  0.64 us (2%)
    pallas_call x1, Pallas kernels, exchange(): pl.pallas_call(functools.partial(exchange_kernel, depth, across, genes),...  38.8 us
    pallas_call x1, Pallas kernels, score(): pl.pallas_call(functools.partial(scores_kernel, scale_factor), grid=(gene...  2.82 us

profile of v3, /device:TPU:0, one launch (start us, length us, event | category | flops | bytes accessed | tf_op | source)
XLA Modules:
  0.0 42.3 jit_solution(7146422545606327075)
XLA Ops:
  0.6 38.8 %shard_map.59 = (bf16[16,32,1280]{2,1,0:T(8,128)(2,1)}, bf16[4,2,2,32,256]{4,3,2,1,0:T(8,128)(2,1)}, bf16[32,256]{1,0:T(8,128)(2,1)}) custom-call(bf16[32,20480]{1,0:T(8,128)(2,1)} %expr_ref.1, bf16[32,256]{1,0:T(8,128)(2,1)} %current_ref.1, s32[16,32]{1,0:T(8,128)} %packed_ref.1, f32[32,64]{1,0:T(8,128)} %cov_ref.1), custom_call_target="tpu_custom_call" | custom-call | tf_op jit(solution)/shard_map/pallas_call | solution.py:282
  39.4 2.8 %shard_map.60 = (f32[1280,256]{1,0:T(8,128)}, bf16[32,256]{1,0:T(8,128)(2,1)}) custom-call(bf16[512,1280]{1,0:T(8,128)(2,1)} %bitcast.2, bf16[512,256]{1,0:T(8,128)(2,1)} %bitcast.3, bf16[32,256]{1,0:T(8,128)(2,1)} %get-tuple-element.7.carried_ref), custom_call_target="tpu_custom_call" | custom-call | tf_op jit(solution)/shard_map/pallas_call | solution.py:323
